TPU v7x, 32 devices: a whole 2x2x4 slice. The times are simulated.
32 devices in a mesh: gx: 4 (over z), gy: 2 (over core), gz: 4 (over y, x).
Axes of the slice: x: 2, y: 2, z: 4, core: 2. Of those that a mesh axis runs over, the one named last changes fastest.
Arguments:
- pair: bfloat16 [128, 512, 512], P('gz', 'gx', 'gy'), may hold values from -6 to 6
- pair_mask: int32 [512, 512], P('gx', 'gy'), may hold values from 0 to 1, as said below
- input_gain: float32 [128], replicated, may hold values from 0.1 to 1.9
- input_weights: bfloat16 [4, 128, 128], replicated, may hold values from -0.5 to 0.5
- out_gate_weight: bfloat16 [128, 128], replicated, may hold values from -0.5 to 0.5
- hidden_gain: float32 [128], replicated, may hold values from 0.1 to 1.9
- out_weight: bfloat16 [128, 128], replicated, may hold values from -0.5 to 0.5
Outputs:
- update: bfloat16 [128, 512, 512], P('gz', 'gx', 'gy')
Inputs may be any that keep to these rules, and one draw needn't show every extreme that they name: pair_mask[r, s] = m[r] * m[s] for a 0/1 residue mask m of the draw that is 0 for all r >= L, for one crop length L with 256 < L <= 512; residues below L may also be 0.
All inputs are finite; a program needn't handle non-finite values.
Results may differ from a plain program's by a relative error of at most 0.011.
Values may be sent and summed in bfloat16 or wider, within the bound.
No kernel may reach another device: no remote copies, remote signals or barrier semaphores. Data moves between devices by JAX's collectives and lax.ppermute only.
A program may use at most 64 MiB of HBM per device.

v0:
```python
import jax
import jax.numpy as jnp
from jax import lax
from jax.sharding import PartitionSpec as P

EPSILON = 1e-05


def own_columns(matrix, width):
    first = lax.axis_index("gz") * width
    return lax.dynamic_slice_in_dim(matrix, first, width, matrix.ndim - 1)


def gated_sides(weights, normed, mask_values, hidden):
    joined = jnp.concatenate([weights[0], weights[1]], axis=1)
    product = jnp.einsum("dk,drs->krs", joined, normed, preferred_element_type=jnp.float32)
    return (mask_values * jax.nn.sigmoid(product[:hidden]) * product[hidden:]).astype(jnp.bfloat16)


def shards(pair, pair_mask, input_gain, input_weights, out_gate_weight, hidden_gain, out_weight):
    local_channels = pair.shape[0]
    all_channels = input_gain.shape[0]
    all_hidden = hidden_gain.shape[0]
    local_hidden = all_hidden // lax.axis_size("gz")
    mask_values = pair_mask.astype(jnp.float32)
    values = pair.astype(jnp.float32)
    moments = lax.psum((jnp.sum(values, axis=0), jnp.sum(values * values, axis=0)), "gz")
    average = moments[0] / all_channels
    spread = moments[1] / all_channels - average * average
    gains = own_columns(input_gain, local_channels)
    normed_local = ((values - average) * lax.rsqrt(spread + EPSILON) * gains[:, None, None]).astype(
        jnp.bfloat16
    )
    normed = lax.all_gather(normed_local, "gz", axis=0, tiled=True)
    side_weights = own_columns(input_weights, local_hidden)
    left_side = gated_sides(side_weights[0:2], normed, mask_values, local_hidden)
    right_side = gated_sides(side_weights[2:4], normed, mask_values, local_hidden)
    gate_weights = own_columns(out_gate_weight, local_channels)
    gate = jax.nn.sigmoid(
        jnp.einsum("dc,drs->crs", gate_weights, normed, preferred_element_type=jnp.float32)
    )
    left_panels = lax.all_gather(left_side, "gy", axis=2, tiled=True)
    row_blocks = lax.all_to_all(left_panels, "gx", split_axis=2, concat_axis=1, tiled=True)
    triangle = jnp.einsum(
        "cki,ckj->icj",
        row_blocks,
        lax.all_gather(right_side, "gx", axis=1, tiled=True),
        preferred_element_type=jnp.float32,
    )
    hidden_gains = own_columns(hidden_gain, local_hidden)
    hidden_stats = lax.psum((jnp.sum(triangle, axis=1), jnp.sum(triangle * triangle, axis=1)), "gz")
    hidden_mean = hidden_stats[0] / all_hidden
    hidden_spread = hidden_stats[1] / all_hidden - hidden_mean * hidden_mean
    hidden_normed = (
        (triangle - hidden_mean[:, None, :])
        * lax.rsqrt(hidden_spread + EPSILON)[:, None, :]
        * hidden_gains[None, :, None]
    ).astype(jnp.bfloat16)
    every_hidden = lax.all_gather(hidden_normed, "gz", axis=1, tiled=True)
    out_columns = own_columns(out_weight, local_channels)
    projected = jnp.einsum(
        "hc,ihj->cij", out_columns, every_hidden, preferred_element_type=jnp.float32
    )
    return (mask_values * gate * projected).astype(jnp.bfloat16)


def solution(mesh):
    placed = (P("gz", "gx", "gy"), P("gx", "gy"), P(), P(), P(), P(), P())
    return jax.shard_map(
        shards, mesh=mesh, in_specs=placed, out_specs=P("gz", "gx", "gy"), check_vma=False
    )
```

profile of v0, /device:TPU:0, one launch (start us, length us, event | category | flops | bytes accessed | tf_op | source)
XLA Modules:
  0.0 593.2 jit_solution(12267018574907195706)
XLA Ops:
  6.5 0.0 copy-start
  6.5 0.0 all-reduce.7.cloned.1.call-start
  6.5 4.8 convert_reduce_fusion
  11.3 0.0 all-reduce.7.cloned.1.call-update
  11.3 0.0 all-gather.5.cloned.1.call-start
  11.4 0.8 dynamic_slice.16
  12.2 45.1 %all-reduce.7.cloned.1.call-done = (f32[128,256]{1,0:T(8,128)}, f32[128,256]{1,0:T(8,128)}) async-done(((f32[128,256]{1,0:T(8,128)}, f32[128,256]{1,0:T(8,128)}), (f32[128,256]{1,0:T(8,128)}, f32[128,256]{1,0:T(8,128)})) %all-reduce.7.cloned.1.call-update) | async-done | bytes 262160 | tf_op jit(solution)/shard_map/psum | solution.py:27
  57.3 1.0 broadcast_multiply_fusion.1
  58.3 3.0 fusion.6
  61.4 0.0 all-gather.5.cloned.1.call-update
  61.4 0.0 all-gather.9.cloned.1.call-start
  61.4 0.1 constant_dynamic-slice_fusion.2
  61.6 0.1 copy.49
  61.6 0.1 copy.50
  61.7 0.1 copy.47
  61.8 0.1 copy.48
  61.9 87.1 %all-gather.5.cloned.1.call-done = bf16[128,128,256]{2,0,1:T(8,128)(2,1)} async-done(((bf16[32,128,256]{2,0,1:T(8,128)(2,1)}), bf16[128,128,256]{2,0,1:T(8,128)(2,1)}) %all-gather.5.cloned.1.call-update) | async-done | bytes 8388624 | tf_op jit(solution)/shard_map/all_gather | solution.py:34
  149.0 4.8 fusion.29
  153.8 1.0 slice-done.1
  154.9 1.3 fusion.26
  156.2 4.1 fusion.13
  160.2 0.0 all-gather.9.cloned.1.call-update
  160.2 0.0 all-gather.7.cloned.1.call-start
  160.3 0.5 all-gather.7.cloned.1.call-update
  160.8 0.0 all-reduce.5.cloned.1.call-start
  160.9 12.3 %all-gather.9.cloned.1.call-done = bf16[32,128,512]{2,0,1:T(8,128)(2,1)} async-done(((bf16[32,128,256]{2,0,1:T(8,128)(2,1)}), bf16[32,128,512]{2,0,1:T(8,128)(2,1)}) %all-gather.9.cloned.1.call-update) | async-done | bytes 4194320 | tf_op jit(solution)/shard_map/all_gather | solution.py:42
  173.2 9.2 %copy.34 = bf16[32,128,512]{1,0,2:T(8,128)(2,1)} copy(bf16[32,128,512]{2,0,1:T(8,128)(2,1)} %all-gather.9.cloned.1.call-done) | data formatting | bytes 8388608 | tf_op jit(solution)/shard_map/all_gather | solution.py:42
  182.3 210.0 %all_to_all.18 = bf16[32,128,512]{1,0,2:T(8,128)(2,1)} all-to-all(bf16[32,128,512]{1,0,2:T(8,128)(2,1)} %copy.34), channel_id=1, replica_groups=mesh['gx'=4,'gy'=2,'gz'=4] {'gx'}, dimensions={2} | all-to-all | bytes 8388608 | tf_op jit(solution)/shard_map/all_to_all | solution.py:43
  392.4 7.6 %copy.35 = bf16[32,128,4,128]{3,1,2,0:T(8,128)(2,1)} copy(bf16[32,128,4,128]{1,0,3,2:T(8,128)(2,1)} %bitcast.40) | data formatting | bytes 8388608 | tf_op jit(solution)/shard_map/all_to_all | solution.py:43
  399.9 14.9 %all-gather.7.cloned.1.call-done = bf16[32,512,256]{2,0,1:T(8,128)(2,1)} async-done(((bf16[32,128,256]{2,0,1:T(8,128)(2,1)}), bf16[32,512,256]{2,0,1:T(8,128)(2,1)}) %all-gather.7.cloned.1.call-update) | async-done | bytes 8388624 | tf_op jit(solution)/shard_map/all_gather | solution.py:47
  414.9 17.5 %bitcast_reduce_fusion = (f32[128,256]{0,1:T(8,128)S(1)}, f32[128,256]{0,1:T(8,128)S(1)}, f32[32,256,128]{2,1,0:T(8,128)}) fusion(bf16[32,512,128]{2,1,0:T(8,128)(2,1)} %bitcast.41, bf16[32,512,256]{2,0,1:T(8,128)(2,1)} %all-gather.7.cloned.1.call-done), kind=kOutput, calls=%fused_computation.27 | convolution fusion | flops 1076822016 | bytes 17039360 | tf_op jit(solution)/shard_map/cki,ckj->icj/dot_general | solution.py:44
  432.4 0.8 copy.37
  433.2 0.8 copy.39
  433.9 0.0 all-reduce.5.cloned.1.call-update
  433.9 0.3 all-gather.11.cloned.1.call-start
  434.2 0.1 dynamic_slice.19
  434.3 41.0 %all-reduce.5.cloned.1.call-done = (f32[128,256]{1,0:T(8,128)}, f32[128,256]{1,0:T(8,128)}) async-done(((f32[128,256]{1,0:T(8,128)}, f32[128,256]{1,0:T(8,128)}), (f32[128,256]{1,0:T(8,128)}, f32[128,256]{1,0:T(8,128)})) %all-reduce.5.cloned.1.call-update) | async-done | bytes 262160 | tf_op jit(solution)/shard_map/psum | solution.py:51
  475.3 1.0 broadcast_multiply_fusion
  476.3 0.1 copy.38
  476.4 0.1 copy.40
  476.5 2.9 fusion.20
  479.4 2.9 copy.41
  482.3 0.0 all-gather.11.cloned.1.call-update
  482.3 0.0 copy-start.4
  482.4 87.6 %all-gather.11.cloned.1.call-done = bf16[128,128,256]{2,0,1:T(8,128)(2,1)} async-done(((bf16[128,32,256]{2,0,1:T(8,128)(2,1)}), bf16[128,128,256]{2,0,1:T(8,128)(2,1)}) %all-gather.11.cloned.1.call-update) | async-done | bytes 8388624 | tf_op jit(solution)/shard_map/all_gather | solution.py:59
  570.0 8.7 %fusion = f32[32,128,256]{2,0,1:T(8,128)S(1)} fusion(bf16[128,128,256]{2,0,1:T(8,128)(2,1)} %all-gather.11.cloned.1.call-done, bf16[128,128]{1,0:T(8,128)(2,1)S(1)} %copy-done, s32[]{:T(128)S(6)} %select_n.2), kind=kOutput, calls=%fused_computation | convolution fusion | flops 268435456 | bytes 12615684 | tf_op jit(solution)/shard_map/hc,ihj->cij/dot_general | solution.py:61
  578.7 5.1 multiply_convert_fusion
  583.8 2.5 copy.43
  (15 shorter events, 0.1 us)
Async XLA Ops:
  6.5 563.4 %copy-start = (bf16[128,128]{1,0:T(8,128)(2,1)S(1)}, bf16[128,128]{1,0:T(8,128)(2,1)}, u32[]{:S(2)}) copy-start(bf16[128,128]{1,0:T(8,128)(2,1)} %param.13) | copy-start | bytes 98308
  6.5 51.8 %copy-start.1 = (bf16[32,128,256]{2,1,0:T(8,128)(2,1)S(1)}, bf16[32,128,256]{2,1,0:T(8,128)(2,1)}, u32[]{:S(2)}) copy-start(bf16[32,128,256]{2,1,0:T(8,128)(2,1)} %param.7) | copy-start | bytes 6291460
  6.5 50.8 %all-reduce.7.cloned.1.call-start = ((), (), s32[]{:S(2)}) async-start(), calls=%async_computation.6 | async-start | bytes 524288 | tf_op jit(solution)/shard_map/psum | solution.py:27
  11.3 50.1 %copy-start.2 = (bf16[4,128,128]{2,1,0:T(8,128)(2,1)S(1)}, bf16[4,128,128]{2,1,0:T(8,128)(2,1)}, u32[]{:S(2)}) copy-start(bf16[4,128,128]{2,1,0:T(8,128)(2,1)} %param.10) | copy-start | bytes 393220
  11.3 50.6 %copy-start.3 = (s32[128,256]{1,0:T(8,128)S(1)}, s32[128,256]{1,0:T(8,128)}, u32[]{:S(2)}) copy-start(s32[128,256]{1,0:T(8,128)} %param.8) | copy-start | bytes 393220
  11.3 137.7 %all-gather.5.cloned.1.call-start = ((), (), s32[]{:S(2)}) async-start(), calls=%async_computation.1 | async-start | bytes 10485760 | tf_op jit(solution)/shard_map/all_gather | solution.py:34
  61.4 111.8 %all-gather.9.cloned.1.call-start = ((), (), s32[]{:S(2)}) async-start(), calls=%async_computation.3 | async-start | bytes 6291456 | tf_op jit(solution)/shard_map/all_gather | solution.py:42
  149.0 4.8 slice-start
  149.0 5.9 slice-start.1
  160.2 254.6 %all-gather.7.cloned.1.call-start = ((), (), s32[]{:S(2)}) async-start(), calls=%async_computation.2 | async-start | bytes 10485760 | tf_op jit(solution)/shard_map/all_gather | solution.py:47
  160.8 314.5 %all-reduce.5.cloned.1.call-start = ((), (), s32[]{:S(2)}) async-start(), calls=%async_computation.5 | async-start | bytes 524288 | tf_op jit(solution)/shard_map/psum | solution.py:51
  414.9 19.4 %copy-start.5 = (f32[128]{0:T(128)S(1)}, f32[128]{0:T(128)}, u32[]{:S(2)}) copy-start(f32[128]{0:T(128)} %param.12) | copy-start | bytes 1540
  433.9 136.0 %all-gather.11.cloned.1.call-start = ((), (), s32[]{:S(2)}) async-start(), calls=%async_computation.4 | async-start | bytes 10485760 | tf_op jit(solution)/shard_map/all_gather | solution.py:59
  482.3 96.3 %copy-start.4 = (bf16[128,128]{1,0:T(8,128)(2,1)S(1)}, bf16[128,128]{1,0:T(8,128)(2,1)}, u32[]{:S(2)}) copy-start(bf16[128,128]{1,0:T(8,128)(2,1)} %param.11) | copy-start | bytes 98308
Sparse Core Ops, SparseCore 0:
  11.5 45.8 all-reduce.6
  61.5 87.4 all-gather.4
  160.4 12.7 all-gather.8
  174.6 240.2 all-gather.6
  434.1 41.2 all-reduce.4
  482.5 87.4 all-gather.10
where the time goes:
time: 594 us; the launch traced here: 593 us
  waiting for transfers between devices  289 us (49%)
  blocking collectives  210 us (35%)
  matrix products  37.5 us (6%)
  local copies, waits for them, and re-layouts  26.2 us (4%)
  other arithmetic  16.8 us (3%)
  between operations  13.6 us (2%)
    all_to_all x1, blocking collectives, shards(): lax.all_to_all(left_panels, 'gx', split_axis=2, concat_axis=1, tiled=True)  210 us
    all_gather x1, waiting for transfers between devices, shards(): every_hidden = lax.all_gather(hidden_normed, 'gz', axis=1, tiled=True)  87.6 us
    all_gather x1, waiting for transfers between devices, shards(): normed = lax.all_gather(normed_local, 'gz', axis=0, tiled=True)  87.1 us
    psum x1, waiting for transfers between devices, shards(): lax.psum((jnp.sum(values, axis=0), jnp.sum(values * values, axis=0)), 'gz')  45.1 us
    psum x1, waiting for transfers between devices, shards(): lax.psum((jnp.sum(triangle, axis=1), jnp.sum(triangle * triangle, axis=1)...  41 us
    dot_general x1, matrix products, shards(): jnp.einsum('cki,ckj->icj', row_blocks, lax.all_gather(right_side, 'gx', a...  17.5 us
    all_gather x1, waiting for transfers between devices, shards(): lax.all_gather(right_side, 'gx', axis=1, tiled=True)  14.9 us
    all_gather x1, waiting for transfers between devices, shards(): left_panels = lax.all_gather(left_side, 'gy', axis=2, tiled=True)  12.3 us
  transfers between devices with their start and end apart: 6, of which 6 were waited for; matrix products, arithmetic and copies ran while one was open for 3% of the time, Pallas kernels for 0%

commit v1 on v0

--- a/solution.py
+++ b/solution.py
@@ -4,6 +4,16 @@
 from jax.sharding import PartitionSpec as P
 
 EPSILON = 1e-05
+
+
+def around_the_ring(x, mesh_axis, d):
+    size = lax.axis_size(mesh_axis)
+    held, blocks = (x, [x])
+    for _ in range(size - 1):
+        held = lax.ppermute(held, mesh_axis, [(i, (i + 1) % size) for i in range(size)])
+        blocks.insert(0, held)
+    flat = jnp.concatenate(blocks, axis=d)
+    return jnp.roll(flat, (lax.axis_index(mesh_axis) + 1) * x.shape[d], axis=d)
 
 
 def own_columns(matrix, width):
@@ -31,7 +41,7 @@
     normed_local = ((values - average) * lax.rsqrt(spread + EPSILON) * gains[:, None, None]).astype(
         jnp.bfloat16
     )
-    normed = lax.all_gather(normed_local, "gz", axis=0, tiled=True)
+    normed = around_the_ring(normed_local, "gz", 0)
     side_weights = own_columns(input_weights, local_hidden)
     left_side = gated_sides(side_weights[0:2], normed, mask_values, local_hidden)
     right_side = gated_sides(side_weights[2:4], normed, mask_values, local_hidden)

time: 594 us -> 662 us (1.11)
  waiting for transfers between devices: 289 us -> 340 us
  local copies, waits for them, and re-layouts: 26.2 us -> 38.3 us
    ppermute x0 -> x3, waiting for transfers between devices: none -> 139 us  [around_the_ring(): lax.ppermute(held, mesh_axis, [(i, (i + 1) % size) for i in range(size)])]
    all_gather x1 -> x0, waiting for transfers between devices: 87.1 us -> none  [shards(): normed = lax.all_gather(normed_local, 'gz', axis=0, tiled=True)]
    unnamed x20 -> x28, local copies, waits for them, and re-layouts: 1.4 us -> 13.6 us
  transfers between devices with their start and end apart: 6 -> 8, of which waited for: 6 -> 8; matrix products, arithmetic and copies ran while one was open for 3% -> 3% of each run, Pallas kernels for 0% -> 0%
where the time goes in v1:
time: 662 us; the launch traced here: 661 us
  waiting for transfers between devices  340 us (51%)
  blocking collectives  210 us (32%)
  local copies, waits for them, and re-layouts  38.3 us (6%)
  matrix products  37.4 us (6%)
  other arithmetic  19 us (3%)
  between operations  13.3 us (2%)
    all_to_all x1, blocking collectives, shards(): lax.all_to_all(left_panels, 'gx', split_axis=2, concat_axis=1, tiled=True)  210 us
    ppermute x3, waiting for transfers between devices, around_the_ring(): lax.ppermute(held, mesh_axis, [(i, (i + 1) % size) for i in range(size)])  139 us
    all_gather x1, waiting for transfers between devices, shards(): every_hidden = lax.all_gather(hidden_normed, 'gz', axis=1, tiled=True)  87.6 us
    psum x1, waiting for transfers between devices, shards(): lax.psum((jnp.sum(values, axis=0), jnp.sum(values * values, axis=0)), 'gz')  45.2 us
    psum x1, waiting for transfers between devices, shards(): lax.psum((jnp.sum(triangle, axis=1), jnp.sum(triangle * triangle, axis=1)...  41 us
    dot_general x1, matrix products, shards(): jnp.einsum('cki,ckj->icj', row_blocks, lax.all_gather(right_side, 'gx', a...  17.6 us
    all_gather x1, waiting for transfers between devices, shards(): lax.all_gather(right_side, 'gx', axis=1, tiled=True)  15 us
    unnamed x28, local copies, waits for them, and re-layouts  13.6 us
  transfers between devices with their start and end apart: 8, of which 8 were waited for; matrix products, arithmetic and copies ran while one was open for 3% of the time, Pallas kernels for 0%

profile of v1, /device:TPU:0, one launch (start us, length us, event | category | flops | bytes accessed | tf_op | source)
XLA Modules:
  0.0 660.9 jit_solution(8496221541052185640)
XLA Ops:
  6.6 4.8 convert_reduce_fusion
  11.4 0.7 dynamic_slice.20
  12.2 45.2 %all-reduce.7.cloned.1.call-done = (f32[128,256]{1,0:T(8,128)}, f32[128,256]{1,0:T(8,128)}) async-done(((f32[128,256]{1,0:T(8,128)}, f32[128,256]{1,0:T(8,128)}), (f32[128,256]{1,0:T(8,128)}, f32[128,256]{1,0:T(8,128)})) %all-reduce.7.cloned.1.call-update) | async-done | bytes 262160 | tf_op jit(solution)/shard_map/psum | solution.py:37
  57.4 1.0 broadcast_multiply_fusion.1
  58.4 1.7 fusion.12
  60.0 1.5 collective-permute-start
  61.6 46.3 %collective-permute-done = bf16[32,128,256]{2,0,1:T(8,128)(2,1)S(1)} collective-permute-done((bf16[32,128,256]{2,0,1:T(8,128)(2,1)S(1)}, bf16[32,128,256]{2,0,1:T(8,128)(2,1)S(1)}, u32[]{:S(2)}, u32[]{:S(2)}) %collective-permute-start) | collective-permute-done | bytes 2097184 | tf_op jit(solution)/shard_map/ppermute | solution.py:13
  107.9 1.3 copy-done.3
  109.2 0.5 collective-permute-start.1
  109.8 46.5 %collective-permute-done.1 = bf16[32,128,256]{2,0,1:T(8,128)(2,1)} collective-permute-done((bf16[32,128,256]{2,0,1:T(8,128)(2,1)S(1)}, bf16[32,128,256]{2,0,1:T(8,128)(2,1)}, u32[]{:S(2)}, u32[]{:S(2)}) %collective-permute-start.1) | collective-permute-done | bytes 2097184 | tf_op jit(solution)/shard_map/ppermute | solution.py:13
  156.2 0.1 constant_dynamic-slice_fusion.2
  156.4 0.1 copy.50
  156.5 0.1 copy.47
  156.6 0.1 copy.48
  156.8 45.9 %collective-permute-done.2 = bf16[32,128,256]{2,0,1:T(8,128)(2,1)} collective-permute-done((bf16[32,128,256]{2,0,1:T(8,128)(2,1)}, bf16[32,128,256]{2,0,1:T(8,128)(2,1)}, u32[]{:S(2)}, u32[]{:S(2)}) %collective-permute-start.2) | collective-permute-done | bytes 2097184 | tf_op jit(solution)/shard_map/ppermute | solution.py:13
  202.6 1.8 constant_dynamic-update-slice_fusion.7
  204.4 1.8 constant_dynamic-update-slice_fusion.6
  206.2 0.2 constant_dynamic-update-slice_fusion.5
  206.4 1.6 constant_dynamic-update-slice_fusion.4
  208.1 1.8 constant_dynamic-update-slice_fusion.3
  209.8 1.8 constant_dynamic-update-slice_fusion.2
  211.6 0.2 constant_dynamic-update-slice_fusion.1
  211.8 1.6 constant_dynamic-update-slice_fusion
  213.5 1.3 fusion.4
  214.8 4.4 copy-done.2
  219.2 4.7 fusion.6
  223.9 4.4 fusion.19
  228.3 0.7 all-gather.4.cloned.1.call-update
  229.1 12.0 %all-gather.6.cloned.1.call-done = bf16[32,128,512]{2,0,1:T(8,128)(2,1)} async-done(((bf16[32,128,256]{2,0,1:T(8,128)(2,1)}), bf16[32,128,512]{2,0,1:T(8,128)(2,1)}) %all-gather.6.cloned.1.call-update) | async-done | bytes 4194320 | tf_op jit(solution)/shard_map/all_gather | solution.py:52
  241.0 9.1 %copy.34 = bf16[32,128,512]{1,0,2:T(8,128)(2,1)} copy(bf16[32,128,512]{2,0,1:T(8,128)(2,1)} %all-gather.6.cloned.1.call-done) | data formatting | bytes 8388608 | tf_op jit(solution)/shard_map/all_gather | solution.py:52
  250.2 210.2 %all_to_all.18 = bf16[32,128,512]{1,0,2:T(8,128)(2,1)} all-to-all(bf16[32,128,512]{1,0,2:T(8,128)(2,1)} %copy.34), channel_id=1, replica_groups=mesh['gx'=4,'gy'=2,'gz'=4] {'gx'}, dimensions={2} | all-to-all | bytes 8388608 | tf_op jit(solution)/shard_map/all_to_all | solution.py:53
  460.4 7.5 %copy.35 = bf16[32,128,4,128]{3,1,2,0:T(8,128)(2,1)} copy(bf16[32,128,4,128]{1,0,3,2:T(8,128)(2,1)} %bitcast.35) | data formatting | bytes 8388608 | tf_op jit(solution)/shard_map/all_to_all | solution.py:53
  467.9 15.0 %all-gather.4.cloned.1.call-done = bf16[32,512,256]{2,0,1:T(8,128)(2,1)} async-done(((bf16[32,128,256]{2,0,1:T(8,128)(2,1)}), bf16[32,512,256]{2,0,1:T(8,128)(2,1)}) %all-gather.4.cloned.1.call-update) | async-done | bytes 8388624 | tf_op jit(solution)/shard_map/all_gather | solution.py:57
  482.9 17.6 %bitcast_reduce_fusion = (f32[128,256]{0,1:T(8,128)S(1)}, f32[128,256]{0,1:T(8,128)S(1)}, f32[32,256,128]{2,1,0:T(8,128)}) fusion(bf16[32,512,128]{2,1,0:T(8,128)(2,1)} %bitcast.36, bf16[32,512,256]{2,0,1:T(8,128)(2,1)} %all-gather.4.cloned.1.call-done), kind=kOutput, calls=%fused_computation.33 | convolution fusion | flops 1076822016 | bytes 17039360 | tf_op jit(solution)/shard_map/cki,ckj->icj/dot_general | solution.py:54
  500.4 0.7 copy.37
  501.2 0.8 copy.39
  502.0 0.3 all-gather.8.cloned.1.call-start
  502.3 0.1 dynamic_slice.24
  502.4 41.0 %all-reduce.5.cloned.1.call-done = (f32[128,256]{1,0:T(8,128)}, f32[128,256]{1,0:T(8,128)}) async-done(((f32[128,256]{1,0:T(8,128)}, f32[128,256]{1,0:T(8,128)}), (f32[128,256]{1,0:T(8,128)}, f32[128,256]{1,0:T(8,128)})) %all-reduce.5.cloned.1.call-update) | async-done | bytes 262160 | tf_op jit(solution)/shard_map/psum | solution.py:61
  543.4 1.0 broadcast_multiply_fusion
  544.4 0.1 copy.38
  544.5 0.1 copy.40
  544.6 2.9 fusion.26
  547.5 2.9 copy.41
  550.4 87.6 %all-gather.8.cloned.1.call-done = bf16[128,128,256]{2,0,1:T(8,128)(2,1)} async-done(((bf16[128,32,256]{2,0,1:T(8,128)(2,1)}), bf16[128,128,256]{2,0,1:T(8,128)(2,1)}) %all-gather.8.cloned.1.call-update) | async-done | bytes 8388624 | tf_op jit(solution)/shard_map/all_gather | solution.py:69
  638.0 8.7 %fusion = f32[32,128,256]{2,0,1:T(8,128)S(1)} fusion(bf16[128,128,256]{2,0,1:T(8,128)(2,1)} %all-gather.8.cloned.1.call-done, bf16[128,128]{1,0:T(8,128)(2,1)S(1)} %copy-done, s32[]{:T(128)S(6)} %select_n.20), kind=kOutput, calls=%fused_computation | convolution fusion | flops 268435456 | bytes 12615684 | tf_op jit(solution)/shard_map/hc,ihj->cij/dot_general | solution.py:71
  646.7 5.2 multiply_convert_fusion
  651.9 2.5 copy.43
  (27 shorter events, 0.4 us)
Async XLA Ops:
  6.5 631.5 %copy-start = (bf16[128,128]{1,0:T(8,128)(2,1)S(1)}, bf16[128,128]{1,0:T(8,128)(2,1)}, u32[]{:S(2)}) copy-start(bf16[128,128]{1,0:T(8,128)(2,1)} %param.13) | copy-start | bytes 98308
  6.5 51.8 %copy-start.1 = (bf16[32,128,256]{2,1,0:T(8,128)(2,1)S(1)}, bf16[32,128,256]{2,1,0:T(8,128)(2,1)}, u32[]{:S(2)}) copy-start(bf16[32,128,256]{2,1,0:T(8,128)(2,1)} %param.7) | copy-start | bytes 6291460
  6.5 149.7 %copy-start.5 = (bf16[4,128,128]{2,1,0:T(8,128)(2,1)S(1)}, bf16[4,128,128]{2,1,0:T(8,128)(2,1)}, u32[]{:S(2)}) copy-start(bf16[4,128,128]{2,1,0:T(8,128)(2,1)} %param.10) | copy-start | bytes 393220
  6.5 150.2 %copy-start.6 = (s32[128,256]{1,0:T(8,128)S(1)}, s32[128,256]{1,0:T(8,128)}, u32[]{:S(2)}) copy-start(s32[128,256]{1,0:T(8,128)} %param.8) | copy-start | bytes 393220
  6.5 50.8 %all-reduce.7.cloned.1.call-start = ((), (), s32[]{:S(2)}) async-start(), calls=%async_computation.5 | async-start | bytes 524288 | tf_op jit(solution)/shard_map/psum | solution.py:37
  11.4 229.6 %all-gather.6.cloned.1.call-start = ((), (), s32[]{:S(2)}) async-start(), calls=%async_computation.2 | async-start | bytes 6291456 | tf_op jit(solution)/shard_map/all_gather | solution.py:52
  60.0 47.8 %collective-permute-start = (bf16[32,128,256]{2,0,1:T(8,128)(2,1)S(1)}, bf16[32,128,256]{2,0,1:T(8,128)(2,1)S(1)}, u32[]{:S(2)}, u32[]{:S(2)}) collective-permute-start(bf16[32,128,256]{2,0,1:T(8,128)(2,1)S(1)} %fusion.12), channel_id=1, source_target_pairs={{0,1},{1,2},{2,3},{3,0},{4,5},{5,6},{6,7},{7,4},{8,9},{9,10},{10,1... | collective-permute-start | bytes 6291464 | tf_op jit(solution)/shard_map/ppermute | solution.py:13
  107.9 1.3 copy-start.3
  109.2 47.0 %collective-permute-start.1 = (bf16[32,128,256]{2,0,1:T(8,128)(2,1)S(1)}, bf16[32,128,256]{2,0,1:T(8,128)(2,1)}, u32[]{:S(2)}, u32[]{:S(2)}) collective-permute-start(bf16[32,128,256]{2,0,1:T(8,128)(2,1)S(1)} %collective-permute-done), channel_id=1, source_target_pairs={{0,1},{1,2},{2,3},{3,0},{4,5},{5,6},{6,7},{7,4},{8,9},{9,10},{10,1... | collective-permute-start | bytes 6291464 | tf_op jit(solution)/shard_map/ppermute | solution.py:13
  156.2 46.4 %collective-permute-start.2 = (bf16[32,128,256]{2,0,1:T(8,128)(2,1)}, bf16[32,128,256]{2,0,1:T(8,128)(2,1)}, u32[]{:S(2)}, u32[]{:S(2)}) collective-permute-start(bf16[32,128,256]{2,0,1:T(8,128)(2,1)} %collective-permute-done.1), channel_id=1, source_target_pairs={{0,1},{1,2},{2,3},{3,0},{4,5},{5,6},{6,7},{7,4},{8,9},{9,10},{10,1... | collective-permute-start | bytes 6291464 | tf_op jit(solution)/shard_map/ppermute | solution.py:13
  156.8 49.4 %copy-start.4 = (bf16[32,128,256]{2,0,1:T(8,128)(2,1)S(1)}, bf16[32,128,256]{2,0,1:T(8,128)(2,1)}, u32[]{:S(2)}) copy-start(bf16[32,128,256]{2,0,1:T(8,128)(2,1)} %copy-done.3) | copy-start | bytes 6291460
  213.5 5.7 copy-start.2
  228.3 254.6 %all-gather.4.cloned.1.call-start = ((), (), s32[]{:S(2)}) async-start(), calls=%async_computation.1 | async-start | bytes 10485760 | tf_op jit(solution)/shard_map/all_gather | solution.py:57
  229.0 314.3 %all-reduce.5.cloned.1.call-start = ((), (), s32[]{:S(2)}) async-start(), calls=%async_computation.4 | async-start | bytes 524288 | tf_op jit(solution)/shard_map/psum | solution.py:61
  482.9 19.4 %copy-start.8 = (f32[128]{0:T(128)S(1)}, f32[128]{0:T(128)}, u32[]{:S(2)}) copy-start(f32[128]{0:T(128)} %param.12) | copy-start | bytes 1540
  502.0 136.0 %all-gather.8.cloned.1.call-start = ((), (), s32[]{:S(2)}) async-start(), calls=%async_computation.3 | async-start | bytes 10485760 | tf_op jit(solution)/shard_map/all_gather | solution.py:69
  550.4 96.3 %copy-start.7 = (bf16[128,128]{1,0:T(8,128)(2,1)S(1)}, bf16[128,128]{1,0:T(8,128)(2,1)}, u32[]{:S(2)}) copy-start(bf16[128,128]{1,0:T(8,128)(2,1)} %param.11) | copy-start | bytes 98308
Sparse Core Ops, SparseCore 0:
  11.5 45.8 all-reduce.6
  228.4 12.5 all-gather.5
  242.6 240.2 all-gather.3
  502.1 41.2 all-reduce.4
  550.5 87.4 all-gather.7
